TPU v7x, 128 devices: a whole 4x4x4 slice. The times are simulated.
128 devices in a mesh: row: 8 (over z, core), col: 16 (over y, x).
Axes of the slice: x: 4, y: 4, z: 4, core: 2. Of those that a mesh axis runs over, the one named last changes fastest.
Arguments:
- coefs: float32 [2, 1536, 16384], P(None, 'row', 'col'), may hold values from -600 to 600, as said below
- tilts: int32 [1536, 2], replicated, may hold values from 8 to 48
- start_basis: float32 [1536, 32], P('col'), may hold values from -6 to 6
Outputs:
- ccc: float32 [1536, 1536], P('row', 'col')
- basis: float32 [1536, 32], P('col')
Inputs may be any that keep to these rules, and one draw needn't show every extreme that they name: `coefs`: real and imaginary parts are products of a particle scale, a coefficient scale and a bounded random value.
All inputs are finite; a program needn't handle non-finite values.
Results may differ from a plain program's by a relative error of at most 0.0003.
Values sent between devices are 32-bit elements; how exact they have to be, the bound alone decides.
A program may use at most 192 MiB of HBM per device.

v0:
```python
import math
import jax
import jax.numpy as jnp
from jax import lax
from jax.sharding import PartitionSpec as P

GRID = 32
ITERS = 4
EPS = 1e-06
HIGH = lax.Precision.HIGHEST


def in_blocks(array, dim, devices):
    before, after = (array.shape[:dim], array.shape[dim + 1 :])
    return jnp.moveaxis(array.reshape(*before, devices, -1, *after), dim, 0)


def sum_at_owner(array, axis, dim):
    tiles = in_blocks(array, dim, lax.axis_size(axis))
    arrived = lax.all_to_all(tiles, axis, split_axis=0, concat_axis=0, tiled=True)
    return arrived.sum(axis=0)


def from_everyone(array, axis):
    copies = jnp.broadcast_to(array, (lax.axis_size(axis), *array.shape))
    return lax.all_to_all(copies, axis, split_axis=0, concat_axis=0, tiled=True)


def over_copies(array, axis):
    return from_everyone(array, axis).sum(axis=0)


def laid_out(tiles, dim):
    dims = list(tiles.shape[1:])
    dims[dim] *= tiles.shape[0]
    return jnp.moveaxis(tiles, 0, dim).reshape(dims)


def gather_directly(array, axis, dim):
    return laid_out(from_everyone(array, axis), dim)


def wedge(tilt_rows, wave_index):
    wave_x = jnp.abs(wave_index // (GRID * (GRID // 2)) - GRID // 2)[None, :]
    wave_z = (wave_index % GRID - GRID // 2)[None, :]
    upward = wave_z * 16 <= tilt_rows[:, 1:2] * wave_x
    downward = -wave_z * 16 <= tilt_rows[:, 0:1] * wave_x
    return jnp.where(wave_z >= 0, upward, downward).astype(jnp.float32)


def inner(left, right):
    return lax.dot_general(
        left, right, (((1,), (1,)), ((), ())), precision=HIGH, preferred_element_type=jnp.float32
    )


def prepare(values, tilt_rows, wave_index):
    masks = wedge(tilt_rows, wave_index)
    paired = jnp.concatenate([values[0] * masks, values[1] * masks], axis=1)
    energy = masks * (values[0] * values[0] + values[1] * values[1])
    return (masks, paired, energy)


def local(coefs, tilts, start_basis):
    row_count = coefs.shape[1]
    slice_width = coefs.shape[2]
    col_count = start_basis.shape[0]
    col_size = lax.axis_size("col")
    total = col_count * col_size
    row_index = lax.axis_index("row")
    col_index = lax.axis_index("col")
    own_tilts = lax.dynamic_slice_in_dim(tilts, row_index * row_count, row_count, 0)
    wave_index = col_index * slice_width + jnp.arange(slice_width, dtype=jnp.int32)
    own_mask, own_pair, own_energy = prepare(coefs, own_tilts, wave_index)
    gathered = lax.all_gather(coefs, "row", axis=1, tiled=True)
    mask_j, pair_j, energy_j = prepare(gathered, tilts, wave_index)
    numer = inner(pair_j, own_pair)
    first = inner(mask_j, own_energy)
    second = inner(energy_j, own_mask)
    summed = sum_at_owner(jnp.concatenate([numer, first, second], axis=1), "col", 0)
    numer = summed[:, :row_count]
    first = summed[:, row_count : 2 * row_count]
    second = summed[:, 2 * row_count :]
    block = (numer / jnp.sqrt(first * second + EPS)).T
    current = start_basis
    for step in range(ITERS):
        partial_value = jnp.dot(block, current, precision=HIGH, preferred_element_type=jnp.float32)
        summed_rows = over_copies(partial_value, "col")
        local_gram = lax.dot_general(
            summed_rows,
            summed_rows,
            (((0,), (0,)), ((), ())),
            precision=HIGH,
            preferred_element_type=jnp.float32,
        )
        gram = over_copies(local_gram, "row")
        factor = jnp.linalg.cholesky(gram)
        fresh = lax.linalg.triangular_solve(
            factor, summed_rows, left_side=False, lower=True, transpose_a=True
        )
        whole = gather_directly(fresh, "row", 0)
        current = lax.dynamic_slice_in_dim(whole, col_index * col_count, col_count, 0)
    return (block, current * math.sqrt(total))


def solution(mesh):
    in_specs = (P(None, "row", "col"), P(), P("col", None))
    out_specs = (P("row", "col"), P("col", None))
    return jax.shard_map(local, mesh=mesh, in_specs=in_specs, out_specs=out_specs, check_vma=False)
```

profile of v0, /device:TPU:1, one launch (start us, length us, event | category | flops | bytes accessed | tf_op | source)
XLA Modules:
  0.0 345.3 jit_solution(13841363534144779767)
XLA Ops:
  7.2 0.7 all-gather.2.cloned.1.call-update
  7.9 0.8 fusion.70
  8.8 0.8 slice_reduce_fusion.1
  9.6 2.9 bitcast_select_fusion.1
  12.5 7.3 %fusion.18 = f32[1536,192]{0,1:T(8,128)} fusion(f32[2,192,1024]{2,1,0:T(8,128)} %param.6, s32[192]{0:T(256)S(1)} %bitcast.109, s32[1024]{0:T(1024)S(1)} %get-tuple-element.21, s32[1024]{0:T(1024)S(1)} %get-tuple-element.20, s32[192]{0:T(256)S(1)} %bitcast.106, s32[1024]{0:T(1024)S(1)} %broadcast_multiply_fusion, ...), kind=kOutput, calls=%fused_computation.29 | convolution fusion | flops 3633512448 | bytes 2797568 | tf_op jit(solution)/shard_map/dot_general | solution.py:52
  19.8 61.0 %all-gather.2.cloned.1.call-done = f32[2,1536,1024]{2,1,0:T(8,128)} async-done(((f32[2,192,1024]{2,1,0:T(8,128)}), f32[2,1536,1024]{2,1,0:T(8,128)}) %all-gather.2.cloned.1.call-update) | async-done | bytes 12582928 | tf_op jit(solution)/shard_map/all_gather | solution.py:75
  80.8 7.4 %fusion.10 = (f32[1536,1024]{1,0:T(8,128)S(1)}, f32[1536,1024]{1,0:T(8,128)S(1)}) fusion(f32[2,1536,1024]{2,1,0:T(8,128)} %all-gather.2.cloned.1.call-done, s32[1536]{0:T(1024)S(1)} %get-tuple-element.13, s32[1024]{0:T(1024)S(1)} %get-tuple-element.21, s32[1024]{0:T(1024)S(1)} %get-tuple-element.20, s32[1536]{0:T(1024)S(1)} %get-tuple-element.12, ...), kind=kLoop, calls=%fused_computation.14 | loop fusion | flops 11010048 | bytes 25191424 | tf_op jit(solution)/shard_map/mul | solution.py:59
  88.2 15.6 %fusion = f32[1536,192]{0,1:T(8,128)} fusion(f32[1536,1024]{1,0:T(8,128)S(1)} %get-tuple-element.15, f32[1536,1024]{1,0:T(8,128)S(1)} %get-tuple-element.14, f32[192,1024]{1,0:T(8,128)} %get-tuple-element.17, f32[192,1024]{1,0:T(8,128)} %get-tuple-element.16), kind=kOutput, calls=%fused_computation | convolution fusion | flops 7251296256 | bytes 15335424 | tf_op jit(solution)/shard_map/dot_general | solution.py:52
  103.9 6.2 %fusion.4 = f32[1536,192]{0,1:T(8,128)S(1)} fusion(f32[2,1536,1024]{2,1,0:T(8,128)S(1)} %bitcast.104, s32[192]{0:T(256)S(1)} %bitcast.110, s32[1024]{0:T(1024)S(1)} %get-tuple-element.21, s32[1024]{0:T(1024)S(1)} %get-tuple-element.20, s32[192]{0:T(256)S(1)} %bitcast.107, s32[1024]{0:T(1024)S(1)} %broadcast_multiply_fusion, ...), kind=kOutput, calls=%fused_computation.6 | convolution fusion | flops 3639017472 | bytes 13807616 | tf_op jit(solution)/shard_map/dot_general | solution.py:52
  110.4 3.1 copy.54
  113.5 54.3 %all_to_all.65 = f32[16,96,576]{2,1,0:T(8,128)} all-to-all(f32[16,96,576]{2,1,0:T(8,128)} %bitcast.102), channel_id=1, replica_groups=mesh['row'=8,'col'=16] {'col'}, dimensions={0} | all-to-all | bytes 7077888 | tf_op jit(solution)/shard_map/all_to_all | solution.py:20
  167.8 2.3 reduce_sum.81
  170.5 13.4 %all_to_all.66 = f32[16,192,32]{1,2,0:T(8,128)S(1)} all-to-all(f32[16,192,32]{1,2,0:T(8,128)S(1)} %broadcast_in_dim.59), channel_id=1, replica_groups=mesh['row'=8,'col'=16] {'col'}, dimensions={0} | all-to-all | bytes 786432 | tf_op jit(solution)/shard_map/all_to_all | solution.py:26
  184.3 10.0 %all_to_all.67 = f32[8,1,1024]{2,1,0:T(1,128)S(1)} all-to-all(f32[8,1,1024]{2,1,0:T(1,128)S(1)} %reshape.98), channel_id=1, replica_groups=mesh['row'=8,'col'=16] {'row'}, dimensions={0} | all-to-all | bytes 65536 | tf_op jit(solution)/shard_map/all_to_all | solution.py:26
  194.8 0.7 reduce.8
  195.7 2.9 cholesky.74
  198.6 0.6 compare_reduce_fusion.3
  199.3 0.7 fusion.27
  199.9 2.4 custom-call.8
  202.6 0.7 broadcast_in_dim.61
  203.3 4.0 %all-to-all-start.3 = ((f32[8,192,32]{1,2,0:T(8,128)}), f32[8,192,32]{1,2,0:T(8,128)S(1)}, u32[]{:S(2)}, u32[]{:S(2)}) async-start(f32[8,192,32]{1,2,0:T(8,128)} %broadcast_in_dim.61), calls=%async_computation.3 | async-start | bytes 524288 | tf_op jit(solution)/shard_map/all_to_all | solution.py:26
  207.4 6.5 %all-to-all-done.3 = f32[8,192,32]{1,2,0:T(8,128)S(1)} async-done(((f32[8,192,32]{1,2,0:T(8,128)}), f32[8,192,32]{1,2,0:T(8,128)S(1)}, u32[]{:S(2)}, u32[]{:S(2)}) %all-to-all-start.3) | async-done | bytes 196640 | tf_op jit(solution)/shard_map/all_to_all | solution.py:26
  214.4 13.0 %all_to_all.68 = f32[16,192,32]{1,2,0:T(8,128)S(1)} all-to-all(f32[16,192,32]{1,2,0:T(8,128)S(1)} %broadcast_in_dim.62), channel_id=1, replica_groups=mesh['row'=8,'col'=16] {'col'}, dimensions={0} | all-to-all | bytes 786432 | tf_op jit(solution)/shard_map/all_to_all | solution.py:26
  227.8 9.2 %all_to_all.69 = f32[8,1,1024]{2,1,0:T(1,128)S(1)} all-to-all(f32[8,1,1024]{2,1,0:T(1,128)S(1)} %reshape.100), channel_id=1, replica_groups=mesh['row'=8,'col'=16] {'row'}, dimensions={0} | all-to-all | bytes 65536 | tf_op jit(solution)/shard_map/all_to_all | solution.py:26
  237.0 0.7 reduce.9
  238.0 2.9 cholesky.85
  241.6 0.7 fusion.28
  242.2 2.4 custom-call.9
  244.9 9.6 %all_to_all.70 = f32[8,192,32]{1,2,0:T(8,128)S(1)} all-to-all(f32[8,192,32]{1,2,0:T(8,128)S(1)} %broadcast_in_dim.64), channel_id=1, replica_groups=mesh['row'=8,'col'=16] {'row'}, dimensions={0} | all-to-all | bytes 393216 | tf_op jit(solution)/shard_map/all_to_all | solution.py:26
  255.1 13.0 %all_to_all.71 = f32[16,192,32]{1,2,0:T(8,128)S(1)} all-to-all(f32[16,192,32]{1,2,0:T(8,128)S(1)} %broadcast_in_dim.65), channel_id=1, replica_groups=mesh['row'=8,'col'=16] {'col'}, dimensions={0} | all-to-all | bytes 786432 | tf_op jit(solution)/shard_map/all_to_all | solution.py:26
  268.5 9.2 %all_to_all.72 = f32[8,1,1024]{2,1,0:T(1,128)S(1)} all-to-all(f32[8,1,1024]{2,1,0:T(1,128)S(1)} %reshape.102), channel_id=1, replica_groups=mesh['row'=8,'col'=16] {'row'}, dimensions={0} | all-to-all | bytes 65536 | tf_op jit(solution)/shard_map/all_to_all | solution.py:26
  277.7 0.7 reduce.10
  278.6 2.9 cholesky.96
  282.2 0.7 fusion.29
  282.9 2.4 custom-call.10
  285.6 9.6 %all_to_all.73 = f32[8,192,32]{1,2,0:T(8,128)S(1)} all-to-all(f32[8,192,32]{1,2,0:T(8,128)S(1)} %broadcast_in_dim.67), channel_id=1, replica_groups=mesh['row'=8,'col'=16] {'row'}, dimensions={0} | all-to-all | bytes 393216 | tf_op jit(solution)/shard_map/all_to_all | solution.py:26
  295.8 13.0 %all_to_all.74 = f32[16,192,32]{1,2,0:T(8,128)S(1)} all-to-all(f32[16,192,32]{1,2,0:T(8,128)S(1)} %broadcast_in_dim.68), channel_id=1, replica_groups=mesh['row'=8,'col'=16] {'col'}, dimensions={0} | all-to-all | bytes 786432 | tf_op jit(solution)/shard_map/all_to_all | solution.py:26
  309.2 9.2 %all_to_all.75 = f32[8,1,1024]{2,1,0:T(1,128)S(1)} all-to-all(f32[8,1,1024]{2,1,0:T(1,128)S(1)} %reshape.104), channel_id=1, replica_groups=mesh['row'=8,'col'=16] {'row'}, dimensions={0} | all-to-all | bytes 65536 | tf_op jit(solution)/shard_map/all_to_all | solution.py:26
  318.4 0.7 reduce.11
  319.3 2.9 cholesky.107
  322.3 0.6 compare_reduce_fusion
  322.9 0.7 fusion.30
  323.6 2.4 custom-call.11
  326.3 0.7 broadcast_in_dim.70
  327.0 4.0 %all-to-all-start.12 = ((f32[8,192,32]{1,2,0:T(8,128)}), f32[8,192,32]{1,2,0:T(8,128)S(1)}, u32[]{:S(2)}, u32[]{:S(2)}) async-start(f32[8,192,32]{1,2,0:T(8,128)} %broadcast_in_dim.70), calls=%async_computation.12 | async-start | bytes 524288 | tf_op jit(solution)/shard_map/all_to_all | solution.py:26
  331.1 0.7 copy.63
  331.9 5.6 %all-to-all-done.12 = f32[8,192,32]{1,2,0:T(8,128)S(1)} async-done(((f32[8,192,32]{1,2,0:T(8,128)}), f32[8,192,32]{1,2,0:T(8,128)S(1)}, u32[]{:S(2)}, u32[]{:S(2)}) %all-to-all-start.12) | async-done | bytes 196640 | tf_op jit(solution)/shard_map/all_to_all | solution.py:26
  337.8 0.7 dynamic-slice_multiply_fusion
  (81 shorter events, 7.7 us)
Async XLA Ops:
  7.2 163.1 %copy-start = (f32[96,32]{0,1:T(8,128)S(1)}, f32[96,32]{0,1:T(8,128)}, u32[]{:S(2)}) copy-start(f32[96,32]{0,1:T(8,128)} %param.8) | copy-start | bytes 36868
  7.2 73.6 %all-gather.2.cloned.1.call-start = ((), (), s32[]{:S(2)}) async-start(), calls=%async_computation.13 | async-start | bytes 14155776 | tf_op jit(solution)/shard_map/all_gather | solution.py:75
  80.8 23.1 %slice-start = ((s8[12582912]{0:T(1024)(128)(4,1)}), s8[4194304]{0:T(1024)(128)(4,1)S(1)}, s32[]{:S(2)}) async-start(s8[12582912]{0:T(1024)(128)(4,1)} %bitcast.103), calls=%async_computation.14 | async-start | bytes 8388608
  80.8 23.1 %slice-start.1 = ((s8[12582912]{0:T(1024)(128)(4,1)}), s8[4194304]{0:T(1024)(128)(4,1)S(1)}, s32[]{:S(2)}) async-start(s8[12582912]{0:T(1024)(128)(4,1)} %bitcast.103), calls=%async_computation.15 | async-start | bytes 8388608
  88.2 15.7 %slice-start.2 = ((s8[12582912]{0:T(1024)(128)(4,1)}), s8[4194304]{0:T(1024)(128)(4,1)S(1)}, s32[]{:S(2)}) async-start(s8[12582912]{0:T(1024)(128)(4,1)} %bitcast.103), calls=%async_computation.16 | async-start | bytes 8388608
  103.9 6.2 %copy-start.1 = (f32[1536,192]{0,1:T(8,128)S(1)}, f32[1536,192]{0,1:T(8,128)}, u32[]{:S(2)}) copy-start(f32[1536,192]{0,1:T(8,128)} %fusion) | copy-start | bytes 3538948
  103.9 6.2 %copy-start.2 = (f32[1536,192]{0,1:T(8,128)S(1)}, f32[1536,192]{0,1:T(8,128)}, u32[]{:S(2)}) copy-start(f32[1536,192]{0,1:T(8,128)} %fusion.18) | copy-start | bytes 3538948
  203.3 10.5 %all-to-all-start.3 = ((f32[8,192,32]{1,2,0:T(8,128)}), f32[8,192,32]{1,2,0:T(8,128)S(1)}, u32[]{:S(2)}, u32[]{:S(2)}) async-start(f32[8,192,32]{1,2,0:T(8,128)} %broadcast_in_dim.61), calls=%async_computation.3 | async-start | bytes 524288 | tf_op jit(solution)/shard_map/all_to_all | solution.py:26
  327.0 10.5 %all-to-all-start.12 = ((f32[8,192,32]{1,2,0:T(8,128)}), f32[8,192,32]{1,2,0:T(8,128)S(1)}, u32[]{:S(2)}, u32[]{:S(2)}) async-start(f32[8,192,32]{1,2,0:T(8,128)} %broadcast_in_dim.70), calls=%async_computation.12 | async-start | bytes 524288 | tf_op jit(solution)/shard_map/all_to_all | solution.py:26
Sparse Core Ops, SparseCore 0:
  9.7 71.0 all-gather.1
where the time goes:
time: 346 us; the launch traced here: 345 us
  blocking collectives  164 us (47%)
  waiting for transfers between devices  73.8 us (21%)
  other arithmetic  43.6 us (13%)
  matrix products  31.7 us (9%)
  between operations  14.5 us (4%)
  local copies, waits for them, and re-layouts  9.96 us (3%)
  starting transfers between devices  8.13 us (2%)
    all_to_all x10, blocking collectives, from_everyone(): return lax.all_to_all(copies, axis, split_axis=0, concat_axis=0, tiled=True)  109 us
    all_gather x1, waiting for transfers between devices, local(): gathered = lax.all_gather(coefs, 'row', axis=1, tiled=True)  61 us
    all_to_all x1, blocking collectives, sum_at_owner(): lax.all_to_all(tiles, axis, split_axis=0, concat_axis=0, tiled=True)  54.3 us
    dot_general x3, matrix products, inner(): lax.dot_general(left, right, (((1,), (1,)), ((), ())), precision=HIGH, pr...  29.2 us
    another operation x12, other arithmetic, local(): factor = jnp.linalg.cholesky(gram)  14.4 us
    another operation x8, other arithmetic, local(): lax.linalg.triangular_solve(factor, summed_rows, left_side=False, lower=T...  12.3 us
    all_to_all x2, waiting for transfers between devices, from_everyone(): return lax.all_to_all(copies, axis, split_axis=0, concat_axis=0, tiled=True)  12.1 us
    mul x2, other arithmetic, prepare(): paired = jnp.concatenate([values[0] * masks, values[1] * masks], axis=1)  10.3 us
  transfers between devices with their start and end apart: 3, of which 3 were waited for; matrix products, arithmetic and copies ran while one was open for 4% of the time, Pallas kernels for 0%

commit v1 on v0

--- a/solution.py
+++ b/solution.py
@@ -3,6 +3,7 @@
 import jax.numpy as jnp
 from jax import lax
 from jax.sharding import PartitionSpec as P
+from jax.lax import all_to_all, axis_size
 
 GRID = 32
 ITERS = 4
@@ -72,7 +73,15 @@
     own_tilts = lax.dynamic_slice_in_dim(tilts, row_index * row_count, row_count, 0)
     wave_index = col_index * slice_width + jnp.arange(slice_width, dtype=jnp.int32)
     own_mask, own_pair, own_energy = prepare(coefs, own_tilts, wave_index)
-    gathered = lax.all_gather(coefs, "row", axis=1, tiled=True)
+    gathered = jnp.concatenate(
+        all_to_all(
+            jnp.stack([coefs for _ in range(axis_size("row"))]),
+            axis_name="row",
+            split_axis=0,
+            concat_axis=0,
+        ),
+        axis=1,
+    )
     mask_j, pair_j, energy_j = prepare(gathered, tilts, wave_index)
     numer = inner(pair_j, own_pair)
     first = inner(mask_j, own_energy)

time: 346 us -> 418 us (1.21)
  waiting for transfers between devices: 73.8 us -> 144 us
  local copies, waits for them, and re-layouts: 9.96 us -> 27.7 us
  between operations: 14.5 us -> 1.09 us
  starting transfers between devices: 8.13 us -> 15 us
  matrix products: 31.7 us -> 25.9 us
    all_to_all x0 -> x1, waiting for transfers between devices: none -> 132 us  [local(): all_to_all(jnp.stack([coefs for _ in range(axis_size('row'))]), axis_name...]
    all_gather x1 -> x0, waiting for transfers between devices: 61 us -> none  [local(): gathered = lax.all_gather(coefs, 'row', axis=1, tiled=True)]
    slice x0 -> x1, local copies, waits for them, and re-layouts: none -> 11.8 us  [prepare(): paired = jnp.concatenate([values[0] * masks, values[1] * masks], axis=1)]
    another operation x0 -> x1, local copies, waits for them, and re-layouts: none -> 7.51 us  [local(): jnp.stack([coefs for _ in range(axis_size('row'))])]
    all_to_all x0 -> x1, starting transfers between devices: none -> 6.93 us  [local(): all_to_all(jnp.stack([coefs for _ in range(axis_size('row'))]), axis_name...]
    dot_general x3, matrix products: 29.2 us -> 23.4 us  [inner(): lax.dot_general(left, right, (((1,), (1,)), ((), ())), precision=HIGH, pr...]
  transfers between devices with their start and end apart: 3 -> 3, of which waited for: 3 -> 3; matrix products, arithmetic and copies ran while one was open for 4% -> 2% of each run, Pallas kernels for 0% -> 0%
where the time goes in v1:
time: 418 us; the launch traced here: 417 us
  blocking collectives  162 us (39%)
  waiting for transfers between devices  144 us (34%)
  other arithmetic  40.7 us (10%)
  local copies, waits for them, and re-layouts  27.7 us (7%)
  matrix products  25.9 us (6%)
  starting transfers between devices  15 us (4%)
    all_to_all x1, waiting for transfers between devices, local(): all_to_all(jnp.stack([coefs for _ in range(axis_size('row'))]), axis_name...  132 us
    all_to_all x10, blocking collectives, from_everyone(): return lax.all_to_all(copies, axis, split_axis=0, concat_axis=0, tiled=True)  109 us
    all_to_all x1, blocking collectives, sum_at_owner(): lax.all_to_all(tiles, axis, split_axis=0, concat_axis=0, tiled=True)  53.3 us
    dot_general x3, matrix products, inner(): lax.dot_general(left, right, (((1,), (1,)), ((), ())), precision=HIGH, pr...  23.4 us
    another operation x12, other arithmetic, local(): factor = jnp.linalg.cholesky(gram)  14.4 us
    another operation x8, other arithmetic, local(): lax.linalg.triangular_solve(factor, summed_rows, left_side=False, lower=T...  12.3 us
    all_to_all x2, waiting for transfers between devices, from_everyone(): return lax.all_to_all(copies, axis, split_axis=0, concat_axis=0, tiled=True)  12.1 us
    slice x1, local copies, waits for them, and re-layouts, prepare(): paired = jnp.concatenate([values[0] * masks, values[1] * masks], axis=1)  11.8 us
  transfers between devices with their start and end apart: 3, of which 3 were waited for; matrix products, arithmetic and copies ran while one was open for 2% of the time, Pallas kernels for 0%

profile of v1, /device:TPU:1, one launch (start us, length us, event | category | flops | bytes accessed | tf_op | source)
XLA Modules:
  0.0 417.0 jit_solution(1593609482043462863)
XLA Ops:
  0.6 7.5 %stack.2 = f32[8,2,192,1024]{3,2,1,0:T(8,128)} broadcast(f32[2,192,1024]{2,1,0:T(8,128)} %param.6), dimensions={1,2,3} | broadcast | bytes 14155776 | tf_op jit(solution)/shard_map/stack | solution.py:78
  8.2 6.9 %all-to-all-start = ((f32[8,2,192,1024]{3,2,1,0:T(8,128)}), f32[8,2,192,1024]{3,2,1,0:T(8,128)}, u32[]{:S(2)}, u32[]{:S(2)}) async-start(f32[8,2,192,1024]{3,2,1,0:T(8,128)} %stack.2), calls=%async_computation | async-start | bytes 25165824 | tf_op jit(solution)/shard_map/all_to_all | solution.py:77
  15.6 6.0 %fusion.12 = f32[1536,192]{0,1:T(8,128)} fusion(f32[2,192,1024]{2,1,0:T(8,128)S(1)} %copy-done.1, s32[192]{0:T(256)S(1)} %bitcast.107, s32[1024]{0:T(1024)S(1)} %get-tuple-element.24, s32[1024]{0:T(1024)S(1)} %get-tuple-element.23, s32[192]{0:T(256)S(1)} %bitcast.104, s32[1024]{0:T(1024)S(1)} %broadcast_multiply_fusion, ...), kind=kOutput, calls=%fused_computation.25 | convolution fusion | flops 3633512448 | bytes 2797568 | tf_op jit(solution)/shard_map/dot_general | solution.py:53
  21.6 132.0 %all-to-all-done = f32[8,2,192,1024]{3,2,1,0:T(8,128)} async-done(((f32[8,2,192,1024]{3,2,1,0:T(8,128)}), f32[8,2,192,1024]{3,2,1,0:T(8,128)}, u32[]{:S(2)}, u32[]{:S(2)}) %all-to-all-start) | async-done | bytes 12582944 | tf_op jit(solution)/shard_map/all_to_all | solution.py:77
  153.6 11.8 %fusion.63 = (f32[1,8,192,1024]{3,2,0,1:T(8,128)}, f32[1,8,192,1024]{3,2,0,1:T(8,128)}) fusion(f32[2,8,192,1024]{3,2,0,1:T(8,128)} %bitcast), kind=kLoop, calls=%fused_computation.107 | loop fusion | bytes 25165824 | tf_op jit(solution)/shard_map/slice | solution.py:60
  165.4 7.0 %bitcast_select_fusion.1 = (f32[1536,1024]{1,0:T(8,128)S(1)}, f32[1536,1024]{1,0:T(8,128)S(1)}, f32[1536,1024]{1,0:T(8,128)S(1)}) fusion(f32[1,8,192,1024]{3,2,0,1:T(8,128)} %get-tuple-element.14, s32[1536]{0:T(1024)S(1)} %get-tuple-element.13, s32[1024]{0:T(1024)S(1)} %get-tuple-element.24, s32[1024]{0:T(1024)S(1)} %get-tuple-element.23, ...), kind=kLoop, calls=%fused_computation.9 | loop fusion | flops 17301504 | bytes 31482880 | tf_op jit(solution)/shard_map/mul | solution.py:60
  172.4 3.9 fusion.59
  176.4 13.5 %fusion = f32[1536,192]{0,1:T(8,128)S(1)} fusion(f32[1536,1024]{1,0:T(8,128)S(1)} %get-tuple-element.18, f32[1536,1024]{1,0:T(8,128)S(1)} %get-tuple-element.16, f32[192,1024]{1,0:T(8,128)S(1)} %get-tuple-element.20, f32[192,1024]{1,0:T(8,128)S(1)} %get-tuple-element.19), kind=kOutput, calls=%fused_computation | convolution fusion | flops 7251296256 | bytes 15335424 | tf_op jit(solution)/shard_map/dot_general | solution.py:53
  190.1 3.1 copy.54
  193.3 53.3 %all_to_all.70 = f32[16,96,576]{2,1,0:T(8,128)} all-to-all(f32[16,96,576]{2,1,0:T(8,128)} %bitcast.102), channel_id=1, replica_groups=mesh['row'=8,'col'=16] {'col'}, dimensions={0} | all-to-all | bytes 7077888 | tf_op jit(solution)/shard_map/all_to_all | solution.py:21
  246.6 2.3 reduce_sum.81
  249.3 12.3 %all_to_all.71 = f32[16,192,32]{1,2,0:T(8,128)S(1)} all-to-all(f32[16,192,32]{1,2,0:T(8,128)S(1)} %broadcast_in_dim.59), channel_id=1, replica_groups=mesh['row'=8,'col'=16] {'col'}, dimensions={0} | all-to-all | bytes 786432 | tf_op jit(solution)/shard_map/all_to_all | solution.py:27
  262.0 10.8 %all_to_all.72 = f32[8,1,1024]{2,1,0:T(1,128)S(1)} all-to-all(f32[8,1,1024]{2,1,0:T(1,128)S(1)} %reshape.109), channel_id=1, replica_groups=mesh['row'=8,'col'=16] {'row'}, dimensions={0} | all-to-all | bytes 65536 | tf_op jit(solution)/shard_map/all_to_all | solution.py:27
  273.3 0.7 reduce.8
  274.2 2.9 cholesky.74
  277.2 0.6 compare_reduce_fusion.3
  277.8 0.7 fusion.21
  278.5 2.4 custom-call.8
  281.2 0.7 broadcast_in_dim.61
  281.9 4.0 all-to-all-start.4
  285.9 6.5 %all-to-all-done.4 = f32[8,192,32]{1,2,0:T(8,128)S(1)} async-done(((f32[8,192,32]{1,2,0:T(8,128)}), f32[8,192,32]{1,2,0:T(8,128)S(1)}, u32[]{:S(2)}, u32[]{:S(2)}) %all-to-all-start.4) | async-done | bytes 196640 | tf_op jit(solution)/shard_map/all_to_all | solution.py:27
  293.0 13.0 %all_to_all.73 = f32[16,192,32]{1,2,0:T(8,128)S(1)} all-to-all(f32[16,192,32]{1,2,0:T(8,128)S(1)} %broadcast_in_dim.62), channel_id=1, replica_groups=mesh['row'=8,'col'=16] {'col'}, dimensions={0} | all-to-all | bytes 786432 | tf_op jit(solution)/shard_map/all_to_all | solution.py:27
  306.4 9.2 %all_to_all.74 = f32[8,1,1024]{2,1,0:T(1,128)S(1)} all-to-all(f32[8,1,1024]{2,1,0:T(1,128)S(1)} %reshape.111), channel_id=1, replica_groups=mesh['row'=8,'col'=16] {'row'}, dimensions={0} | all-to-all | bytes 65536 | tf_op jit(solution)/shard_map/all_to_all | solution.py:27
  315.6 0.7 reduce.9
  316.5 2.9 cholesky.85
  319.5 0.6 compare_reduce_fusion.2
  320.1 0.7 fusion.22
  320.8 2.4 custom-call.9
  323.5 9.6 %all_to_all.75 = f32[8,192,32]{1,2,0:T(8,128)S(1)} all-to-all(f32[8,192,32]{1,2,0:T(8,128)S(1)} %broadcast_in_dim.64), channel_id=1, replica_groups=mesh['row'=8,'col'=16] {'row'}, dimensions={0} | all-to-all | bytes 393216 | tf_op jit(solution)/shard_map/all_to_all | solution.py:27
  333.7 13.0 %all_to_all.76 = f32[16,192,32]{1,2,0:T(8,128)S(1)} all-to-all(f32[16,192,32]{1,2,0:T(8,128)S(1)} %broadcast_in_dim.65), channel_id=1, replica_groups=mesh['row'=8,'col'=16] {'col'}, dimensions={0} | all-to-all | bytes 786432 | tf_op jit(solution)/shard_map/all_to_all | solution.py:27
  347.1 9.2 %all_to_all.77 = f32[8,1,1024]{2,1,0:T(1,128)S(1)} all-to-all(f32[8,1,1024]{2,1,0:T(1,128)S(1)} %reshape.113), channel_id=1, replica_groups=mesh['row'=8,'col'=16] {'row'}, dimensions={0} | all-to-all | bytes 65536 | tf_op jit(solution)/shard_map/all_to_all | solution.py:27
  356.3 0.7 reduce.10
  357.2 2.9 cholesky.96
  360.2 0.6 compare_reduce_fusion.1
  360.8 0.7 fusion.23
  361.5 2.4 custom-call.10
  364.2 9.6 %all_to_all.78 = f32[8,192,32]{1,2,0:T(8,128)S(1)} all-to-all(f32[8,192,32]{1,2,0:T(8,128)S(1)} %broadcast_in_dim.67), channel_id=1, replica_groups=mesh['row'=8,'col'=16] {'row'}, dimensions={0} | all-to-all | bytes 393216 | tf_op jit(solution)/shard_map/all_to_all | solution.py:27
  374.4 13.0 %all_to_all.79 = f32[16,192,32]{1,2,0:T(8,128)S(1)} all-to-all(f32[16,192,32]{1,2,0:T(8,128)S(1)} %broadcast_in_dim.68), channel_id=1, replica_groups=mesh['row'=8,'col'=16] {'col'}, dimensions={0} | all-to-all | bytes 786432 | tf_op jit(solution)/shard_map/all_to_all | solution.py:27
  387.7 9.2 %all_to_all.80 = f32[8,1,1024]{2,1,0:T(1,128)S(1)} all-to-all(f32[8,1,1024]{2,1,0:T(1,128)S(1)} %reshape.115), channel_id=1, replica_groups=mesh['row'=8,'col'=16] {'row'}, dimensions={0} | all-to-all | bytes 65536 | tf_op jit(solution)/shard_map/all_to_all | solution.py:27
  397.0 0.7 reduce.11
  397.9 2.9 cholesky.107
  401.5 0.7 fusion.24
  402.1 2.4 custom-call.11
  404.8 0.7 broadcast_in_dim.70
  405.5 4.0 all-to-all-start.13
  409.7 0.7 copy.63
  410.4 5.6 %all-to-all-done.13 = f32[8,192,32]{1,2,0:T(8,128)S(1)} async-done(((f32[8,192,32]{1,2,0:T(8,128)}), f32[8,192,32]{1,2,0:T(8,128)S(1)}, u32[]{:S(2)}, u32[]{:S(2)}) %all-to-all-start.13) | async-done | bytes 196640 | tf_op jit(solution)/shard_map/all_to_all | solution.py:27
  416.4 0.7 dynamic-slice_multiply_fusion
  (77 shorter events, 7.5 us)
Async XLA Ops:
  0.6 248.4 %copy-start = (f32[96,32]{0,1:T(8,128)S(1)}, f32[96,32]{0,1:T(8,128)}, u32[]{:S(2)}) copy-start(f32[96,32]{0,1:T(8,128)} %param.8) | copy-start | bytes 36868
  8.2 7.0 %copy-start.3 = (s32[1536,2]{0,1:T(2,128)S(1)}, s32[1536,2]{0,1:T(2,128)}, u32[]{:S(2)}) copy-start(s32[1536,2]{0,1:T(2,128)} %param.7) | copy-start | bytes 36868
  8.2 7.1 %copy-start.1 = (f32[2,192,1024]{2,1,0:T(8,128)S(1)}, f32[2,192,1024]{2,1,0:T(8,128)}, u32[]{:S(2)}) copy-start(f32[2,192,1024]{2,1,0:T(8,128)} %param.6) | copy-start | bytes 4718596
  8.2 145.5 %all-to-all-start = ((f32[8,2,192,1024]{3,2,1,0:T(8,128)}), f32[8,2,192,1024]{3,2,1,0:T(8,128)}, u32[]{:S(2)}, u32[]{:S(2)}) async-start(f32[8,2,192,1024]{3,2,1,0:T(8,128)} %stack.2), calls=%async_computation | async-start | bytes 25165824 | tf_op jit(solution)/shard_map/all_to_all | solution.py:77
  176.3 13.5 %copy-start.2 = (f32[1536,192]{0,1:T(8,128)S(1)}, f32[1536,192]{0,1:T(8,128)}, u32[]{:S(2)}) copy-start(f32[1536,192]{0,1:T(8,128)} %fusion.12) | copy-start | bytes 3538948
  281.9 10.5 %all-to-all-start.4 = ((f32[8,192,32]{1,2,0:T(8,128)}), f32[8,192,32]{1,2,0:T(8,128)S(1)}, u32[]{:S(2)}, u32[]{:S(2)}) async-start(f32[8,192,32]{1,2,0:T(8,128)} %broadcast_in_dim.61), calls=%async_computation.4 | async-start | bytes 524288 | tf_op jit(solution)/shard_map/all_to_all | solution.py:27
  405.5 10.5 %all-to-all-start.13 = ((f32[8,192,32]{1,2,0:T(8,128)}), f32[8,192,32]{1,2,0:T(8,128)S(1)}, u32[]{:S(2)}, u32[]{:S(2)}) async-start(f32[8,192,32]{1,2,0:T(8,128)} %broadcast_in_dim.70), calls=%async_computation.13 | async-start | bytes 524288 | tf_op jit(solution)/shard_map/all_to_all | solution.py:27
